TPU v7x, 32 devices: a whole 2x2x4 slice. The times are simulated.
32 devices in a mesh: dp: 4 (over y, x), vocab: 8 (over z, core).
Axes of the slice: x: 2, y: 2, z: 4, core: 2. Of those that a mesh axis runs over, the one named last changes fastest.
Arguments:
- hidden: bfloat16 [1024, 8192], P('dp'), may hold values from -14 to 14
- weight: bfloat16 [8192, 8192], P('dp', 'vocab'), may hold values from -1 to 1, as said below
- targets: int32 [1024], P('dp'), may hold values from 0 to 8191
- cotangent: float32 [1024], P('dp'), may hold values from 1 to 8
Outputs:
- loss: float32 [1024], P('dp')
- grad_hidden: bfloat16 [1024, 8192], P('vocab', 'dp')
- grad_weight: bfloat16 [8192, 8192], P('dp', 'vocab')
Inputs may be any that keep to these rules, and one draw needn't show every extreme that they name: `weight`: entries drawn with standard deviation 4 / sqrt(8192).
All inputs are finite; a program needn't handle non-finite values.
Results may differ from a plain program's by a relative error of at most 0.0047.
Values may be sent and summed in bfloat16 or wider, within the bound.
No kernel may reach another device: no remote copies, remote signals or barrier semaphores. Data moves between devices by JAX's collectives and lax.ppermute only.
A program may use at most 128 MiB of HBM per device.

v0:
```python
import jax
import jax.numpy as jnp
from jax import lax
from jax.sharding import PartitionSpec as P


def shards(hidden, weight, targets, cotangent):
    vocab_width = weight.shape[1]
    spread = lax.all_to_all(hidden, "dp", split_axis=1, concat_axis=0, tiled=True)
    vocab_first = lax.axis_index("vocab") * vocab_width
    columns = vocab_first + lax.iota(jnp.int32, vocab_width)
    onehot = (targets[:, None] == columns[None, :]).astype(jnp.float32)
    row_block = spread
    logits = lax.psum_scatter(
        jnp.dot(row_block, weight, preferred_element_type=jnp.float32),
        "dp",
        scatter_dimension=0,
        tiled=True,
    )
    local_max = jnp.max(logits, axis=1)
    local_pick = jnp.sum(logits * onehot, axis=1)
    row_max = lax.pmax(local_max, "vocab")
    shifted = jnp.exp(logits - row_max[:, None])
    sum_exp, picked = lax.psum((jnp.sum(shifted, axis=1), local_pick), "vocab")
    loss = row_max + jnp.log(sum_exp) - picked
    grad_logits = (cotangent[:, None] * (shifted / sum_exp[:, None] - onehot)).astype(jnp.bfloat16)
    all_grads = lax.all_gather(grad_logits, "dp", axis=0, tiled=True)
    grad_weight = lax.dot_general(
        spread, all_grads, (((0,), (0,)), ((), ())), preferred_element_type=jnp.float32
    ).astype(jnp.bfloat16)
    row_block = all_grads
    grad_hidden = lax.psum_scatter(
        lax.dot_general(
            row_block, weight, (((1,), (1,)), ((), ())), preferred_element_type=jnp.float32
        ),
        "vocab",
        scatter_dimension=0,
        tiled=True,
    ).astype(jnp.bfloat16)
    return (loss, grad_hidden, grad_weight)


def solution(mesh):
    in_specs = (P("dp", None), P("dp", "vocab"), P("dp"), P("dp"))
    out_specs = (P("dp"), P("vocab", "dp"), P("dp", "vocab"))
    return jax.shard_map(shards, mesh=mesh, in_specs=in_specs, out_specs=out_specs, check_vma=False)
```

profile of v0, /device:TPU:0, one launch (start us, length us, event | category | flops | bytes accessed | tf_op | source)
XLA Modules:
  0.0 314.0 jit_solution(2251081179240819122)
XLA Ops:
  7.2 0.0 reduce-scatter.3.cloned.1.call-start
  7.2 6.4 %copy.9 = bf16[256,8192]{0,1:T(8,128)(2,1)} copy(bf16[256,8192]{1,0:T(8,128)(2,1)} %param.4) | data formatting | bytes 8388608 | tf_op args[0]
  13.6 55.1 %all_to_all.19 = bf16[256,4,2048]{0,2,1:T(8,128)(2,1)} all-to-all(bf16[256,4,2048]{0,2,1:T(8,128)(2,1)} %bitcast.12), channel_id=1, replica_groups=mesh['dp'=4,'vocab'=8] {'dp'}, dimensions={1} | all-to-all | bytes 8388608 | tf_op jit(solution)/shard_map/all_to_all | solution.py:9
  68.7 6.2 %copy.10 = bf16[4,256,2048]{2,1,0:T(8,128)(2,1)} copy(bf16[4,256,2048]{1,2,0:T(8,128)(2,1)} %bitcast.11) | data formatting | bytes 8388608 | tf_op jit(solution)/shard_map/all_to_all | solution.py:9
  74.9 9.9 %fusion.5 = f32[1024,1024]{1,0:T(8,128)} fusion(bf16[1024,2048]{1,0:T(8,128)(2,1)} %bitcast.13, bf16[2048,1024]{1,0:T(8,128)(2,1)} %param.5), kind=kOutput, calls=%fused_computation.11 | convolution fusion | flops 4294967296 | bytes 12582912 | tf_op jit(solution)/shard_map/dot_general | solution.py:15
  84.8 0.0 reduce-scatter.3.cloned.1.call-update
  84.8 0.0 all-gather.2.cloned.1.call-start
  84.8 52.6 %reduce-scatter.3.cloned.1.call-done = f32[256,1024]{1,0:T(8,128)} async-done(((f32[1024,1024]{1,0:T(8,128)}), f32[256,1024]{1,0:T(8,128)}) %reduce-scatter.3.cloned.1.call-update) | async-done | bytes 1048592 | tf_op jit(solution)/shard_map/reduce_scatter | solution.py:14
  137.4 1.4 reduce_max.9
  138.8 16.2 %pmax.7 = f32[256]{0:T(256)S(1)} all-reduce(f32[256]{0:T(256)S(1)} %reduce_max.9), channel_id=1, replica_groups=mesh['dp'=4,'vocab'=8] {'vocab'}, use_global_device_ids=true, to_apply=%region_2.0 | all-reduce | flops 256 | bytes 2048 | tf_op jit(solution)/shard_map/pmax | solution.py:22
  155.0 1.6 fusion.4
  156.6 13.6 %all-reduce = (f32[256]{0:T(256)S(1)}, f32[256]{0:T(256)S(1)}) all-reduce(f32[256]{0:T(256)S(1)} %get-tuple-element.13, f32[256]{0:T(256)S(1)} %get-tuple-element.12), channel_id=1, replica_groups=mesh['dp'=4,'vocab'=8] {'vocab'}, use_global_device_ids=true, to_apply=%region_6.0 | all-reduce | flops 512 | bytes 4096 | tf_op jit(solution)/shard_map/psum | solution.py:24
  170.2 2.4 fusion.3
  172.6 0.0 all-gather.2.cloned.1.call-update
  172.6 0.0 reduce-scatter.5.cloned.1.call-start
  172.6 32.5 %all-gather.2.cloned.1.call-done = bf16[1024,1024]{1,0:T(8,128)(2,1)} async-done(((bf16[256,1024]{1,0:T(8,128)(2,1)}), bf16[1024,1024]{1,0:T(8,128)(2,1)}) %all-gather.2.cloned.1.call-update) | async-done | bytes 2097168 | tf_op jit(solution)/shard_map/all_gather | solution.py:27
  205.1 10.6 %fusion.6 = f32[1024,2048]{1,0:T(8,128)} fusion(bf16[1024,1024]{1,0:T(8,128)(2,1)} %all-gather.2.cloned.1.call-done, bf16[2048,1024]{1,0:T(8,128)(2,1)} %param.5), kind=kOutput, calls=%fused_computation.12 | convolution fusion | flops 4294967296 | bytes 14680064 | tf_op jit(solution)/shard_map/dot_general | solution.py:33
  215.7 0.0 reduce-scatter.5.cloned.1.call-update
  215.7 0.6 add_subtract_fusion
  216.3 1.0 copy-done.2
  217.3 8.3 %convert_bitcast_fusion = bf16[2048,1024]{0,1:T(8,128)(2,1)} fusion(bf16[1024,1024]{1,0:T(8,128)(2,1)S(1)} %copy-done.2, bf16[1024,2048]{1,0:T(8,128)(2,1)} %bitcast.14), kind=kOutput, calls=%fused_computation | convolution fusion | flops 4297064448 | bytes 10485760 | tf_op jit(solution)/shard_map/dot_general | solution.py:28
  225.6 6.4 %copy.11 = bf16[2048,1024]{1,0:T(8,128)(2,1)} copy(bf16[2048,1024]{0,1:T(8,128)(2,1)} %convert_bitcast_fusion) | data formatting | bytes 8388608
  232.0 73.4 %reduce-scatter.5.cloned.1.call-done = f32[128,2048]{1,0:T(8,128)} async-done(((f32[1024,2048]{1,0:T(8,128)}), f32[128,2048]{1,0:T(8,128)}) %reduce-scatter.5.cloned.1.call-update) | async-done | bytes 1048592 | tf_op jit(solution)/shard_map/reduce_scatter | solution.py:32
  305.4 2.1 convert_element_type.17
  (6 shorter events, 0.0 us)
Async XLA Ops:
  7.2 130.3 %reduce-scatter.3.cloned.1.call-start = ((), (), s32[]{:S(2)}) async-start(), calls=%async_computation.3 | async-start | bytes 5242880 | tf_op jit(solution)/shard_map/reduce_scatter | solution.py:14
  84.7 70.2 %copy-start = (s32[256]{0:T(256)S(1)}, s32[256]{0:T(256)}, u32[]{:S(2)}) copy-start(s32[256]{0:T(256)} %param.6) | copy-start | bytes 3076
  84.8 85.4 %copy-start.1 = (f32[256]{0:T(256)S(1)}, f32[256]{0:T(256)}, u32[]{:S(2)}) copy-start(f32[256]{0:T(256)} %param.7) | copy-start | bytes 3076
  84.8 120.4 %all-gather.2.cloned.1.call-start = ((), (), s32[]{:S(2)}) async-start(), calls=%async_computation.4 | async-start | bytes 2621440 | tf_op jit(solution)/shard_map/all_gather | solution.py:27
  172.6 132.9 %reduce-scatter.5.cloned.1.call-start = ((), (), s32[]{:S(2)}) async-start(), calls=%async_computation.5 | async-start | bytes 9437184 | tf_op jit(solution)/shard_map/reduce_scatter | solution.py:32
  215.7 1.6 copy-start.2
Sparse Core Ops, SparseCore 0:
  84.9 52.4 reduce-scatter.2
  172.7 32.3 all-gather.1
  215.9 89.5 reduce-scatter.4
where the time goes:
time: 315 us; the launch traced here: 314 us
  waiting for transfers between devices  159 us (50%)
  blocking collectives  84.9 us (27%)
  matrix products  28.7 us (9%)
  local copies, waits for them, and re-layouts  20 us (6%)
  between operations  13.8 us (4%)
  other arithmetic  8 us (3%)
    reduce_scatter x1, waiting for transfers between devices, shards(): lax.psum_scatter(lax.dot_general(row_block, weight, (((1,), (1,)), ((), (...  73.4 us
    all_to_all x1, blocking collectives, shards(): lax.all_to_all(hidden, 'dp', split_axis=1, concat_axis=0, tiled=True)  55.1 us
    reduce_scatter x1, waiting for transfers between devices, shards(): lax.psum_scatter(jnp.dot(row_block, weight, preferred_element_type=jnp.fl...  52.6 us
    all_gather x1, waiting for transfers between devices, shards(): all_grads = lax.all_gather(grad_logits, 'dp', axis=0, tiled=True)  32.5 us
    pmax x1, blocking collectives, shards(): row_max = lax.pmax(local_max, 'vocab')  16.2 us
    unnamed x8, local copies, waits for them, and re-layouts  13.8 us
    psum x1, blocking collectives, shards(): sum_exp, picked = lax.psum((jnp.sum(shifted, axis=1), local_pick), 'vocab')  13.6 us
    dot_general x1, matrix products, shards(): lax.dot_general(row_block, weight, (((1,), (1,)), ((), ())), preferred_el...  10.6 us
  transfers between devices with their start and end apart: 3, of which 3 were waited for; matrix products, arithmetic and copies ran while one was open for 5% of the time, Pallas kernels for 0%

commit v1 on v0

--- a/solution.py
+++ b/solution.py
@@ -6,7 +6,10 @@
 
 def shards(hidden, weight, targets, cotangent):
     vocab_width = weight.shape[1]
-    spread = lax.all_to_all(hidden, "dp", split_axis=1, concat_axis=0, tiled=True)
+    spread = jnp.concatenate(
+        lax.all_to_all(jnp.stack(jnp.split(hidden, lax.axis_size("dp"), axis=1)), "dp", 0, 0),
+        axis=0,
+    )
     vocab_first = lax.axis_index("vocab") * vocab_width
     columns = vocab_first + lax.iota(jnp.int32, vocab_width)
     onehot = (targets[:, None] == columns[None, :]).astype(jnp.float32)

time: 315 us -> 301 us (0.956)
  local copies, waits for them, and re-layouts: 20 us -> 5.74 us
  waiting for transfers between devices: 159 us -> 165 us
  matrix products: 28.7 us -> 24.9 us
    unnamed x8 -> x10, local copies, waits for them, and re-layouts: 13.8 us -> 2.98 us
    reduce_scatter x1, waiting for transfers between devices: 73.4 us -> 79.8 us  [shards(): lax.psum_scatter(lax.dot_general(row_block, weight, (((1,), (1,)), ((), (...]
    all_to_all x1 -> x0, local copies, waits for them, and re-layouts: 6.19 us -> none  [shards(): lax.all_to_all(hidden, 'dp', split_axis=1, concat_axis=0, tiled=True)]
    dot_general x1, matrix products: 9.88 us -> 6.01 us  [shards(): jnp.dot(row_block, weight, preferred_element_type=jnp.float32)]
  transfers between devices with their start and end apart: 3 -> 3, of which waited for: 3 -> 3; matrix products, arithmetic and copies ran while one was open for 5% -> 3% of each run, Pallas kernels for 0% -> 0%
where the time goes in v1:
time: 301 us
  waiting for transfers between devices  165 us (55%)
  blocking collectives  82.9 us (28%)
  matrix products  24.9 us (8%)
  between operations  13.8 us (5%)
  other arithmetic  8.57 us (3%)
  local copies, waits for them, and re-layouts  5.74 us (2%)
    reduce_scatter x1, waiting for transfers between devices, shards(): lax.psum_scatter(lax.dot_general(row_block, weight, (((1,), (1,)), ((), (...  79.8 us
    all_to_all x1, blocking collectives, shards(): lax.all_to_all(jnp.stack(jnp.split(hidden, lax.axis_size('dp'), axis=1)),...  53.1 us
    reduce_scatter x1, waiting for transfers between devices, shards(): lax.psum_scatter(jnp.dot(row_block, weight, preferred_element_type=jnp.fl...  52.4 us
    all_gather x1, waiting for transfers between devices, shards(): all_grads = lax.all_gather(grad_logits, 'dp', axis=0, tiled=True)  32.5 us
    pmax x1, blocking collectives, shards(): row_max = lax.pmax(local_max, 'vocab')  16.2 us
    psum x1, blocking collectives, shards(): sum_exp, picked = lax.psum((jnp.sum(shifted, axis=1), local_pick), 'vocab')  13.6 us
    dot_general x1, matrix products, shards(): lax.dot_general(row_block, weight, (((1,), (1,)), ((), ())), preferred_el...  10.6 us
    dot_general x1, matrix products, shards(): lax.dot_general(spread, all_grads, (((0,), (0,)), ((), ())), preferred_el...  8.3 us
  transfers between devices with their start and end apart: 3, of which 3 were waited for; matrix products, arithmetic and copies ran while one was open for 3% of the time, Pallas kernels for 0%

profile of v1, /device:TPU:0, one launch (start us, length us, event | category | flops | bytes accessed | tf_op | source)
XLA Modules:
  0.0 300.8 jit_solution(15217701985205269333)
XLA Ops:
  7.2 0.0 reduce-scatter.3.cloned.1.call-start
  7.2 2.8 slice_bitcast_fusion.3
  10.0 0.6 pad_maximum_fusion
  10.6 53.1 %all_to_all.5 = bf16[4,256,2048]{2,1,0:T(8,128)(2,1)S(1)} all-to-all(bf16[4,256,2048]{2,1,0:T(8,128)(2,1)S(1)} %pad_maximum_fusion), channel_id=1, replica_groups=mesh['dp'=4,'vocab'=8] {'dp'}, dimensions={0} | all-to-all | bytes 8388608 | tf_op jit(solution)/shard_map/all_to_all | solution.py:10
  63.7 2.0 copy-done
  65.6 6.0 %fusion.5 = f32[1024,1024]{1,0:T(8,128)} fusion(bf16[1024,2048]{1,0:T(8,128)(2,1)S(1)} %bitcast.15, bf16[2048,1024]{1,0:T(8,128)(2,1)S(1)} %copy-done.3), kind=kOutput, calls=%fused_computation.16 | convolution fusion | flops 4294967296 | bytes 12582912 | tf_op jit(solution)/shard_map/dot_general | solution.py:18
  71.7 0.0 reduce-scatter.3.cloned.1.call-update
  71.7 0.0 all-gather.2.cloned.1.call-start
  71.7 52.4 %reduce-scatter.3.cloned.1.call-done = f32[256,1024]{1,0:T(8,128)} async-done(((f32[1024,1024]{1,0:T(8,128)}), f32[256,1024]{1,0:T(8,128)}) %reduce-scatter.3.cloned.1.call-update) | async-done | bytes 1048592 | tf_op jit(solution)/shard_map/reduce_scatter | solution.py:17
  124.1 1.4 reduce_max.9
  125.5 16.2 %pmax.7 = f32[256]{0:T(256)S(1)} all-reduce(f32[256]{0:T(256)S(1)} %reduce_max.9), channel_id=1, replica_groups=mesh['dp'=4,'vocab'=8] {'vocab'}, use_global_device_ids=true, to_apply=%region_2.0 | all-reduce | flops 256 | bytes 2048 | tf_op jit(solution)/shard_map/pmax | solution.py:25
  141.7 1.6 fusion.4
  143.3 13.6 %all-reduce = (f32[256]{0:T(256)S(1)}, f32[256]{0:T(256)S(1)}) all-reduce(f32[256]{0:T(256)S(1)} %get-tuple-element.4, f32[256]{0:T(256)S(1)} %get-tuple-element.3), channel_id=1, replica_groups=mesh['dp'=4,'vocab'=8] {'vocab'}, use_global_device_ids=true, to_apply=%region_6.0 | all-reduce | flops 512 | bytes 4096 | tf_op jit(solution)/shard_map/psum | solution.py:27
  156.9 2.4 fusion.3
  159.3 0.0 all-gather.2.cloned.1.call-update
  159.3 0.0 reduce-scatter.5.cloned.1.call-start
  159.4 32.5 %all-gather.2.cloned.1.call-done = bf16[1024,1024]{1,0:T(8,128)(2,1)} async-done(((bf16[256,1024]{1,0:T(8,128)(2,1)}), bf16[1024,1024]{1,0:T(8,128)(2,1)}) %all-gather.2.cloned.1.call-update) | async-done | bytes 2097168 | tf_op jit(solution)/shard_map/all_gather | solution.py:30
  191.9 10.6 %fusion.6 = f32[1024,2048]{1,0:T(8,128)} fusion(bf16[1024,1024]{1,0:T(8,128)(2,1)} %all-gather.2.cloned.1.call-done, bf16[2048,1024]{1,0:T(8,128)(2,1)} %param.5), kind=kOutput, calls=%fused_computation.17 | convolution fusion | flops 4294967296 | bytes 14680064 | tf_op jit(solution)/shard_map/dot_general | solution.py:36
  202.4 0.0 reduce-scatter.5.cloned.1.call-update
  202.5 0.6 add_subtract_fusion
  203.0 1.0 copy-done.4
  204.0 8.3 %convolution_convert_fusion = bf16[2048,1024]{1,0:T(8,128)(2,1)} fusion(bf16[1024,2048]{1,0:T(8,128)(2,1)} %bitcast.16, bf16[1024,1024]{1,0:T(8,128)(2,1)S(1)} %copy-done.4), kind=kOutput, calls=%fused_computation.1 | convolution fusion | flops 4297064448 | bytes 10485760 | tf_op jit(solution)/shard_map/dot_general | solution.py:31
  212.3 79.8 %reduce-scatter.5.cloned.1.call-done = f32[128,2048]{1,0:T(8,128)} async-done(((f32[1024,2048]{1,0:T(8,128)}), f32[128,2048]{1,0:T(8,128)}) %reduce-scatter.5.cloned.1.call-update) | async-done | bytes 1048592 | tf_op jit(solution)/shard_map/reduce_scatter | solution.py:35
  292.1 2.1 convert_element_type.14
  (9 shorter events, 0.0 us)
Async XLA Ops:
  7.2 117.0 %reduce-scatter.3.cloned.1.call-start = ((), (), s32[]{:S(2)}) async-start(), calls=%async_computation.3 | async-start | bytes 5242880 | tf_op jit(solution)/shard_map/reduce_scatter | solution.py:17
  10.6 55.1 %copy-start.3 = (bf16[2048,1024]{1,0:T(8,128)(2,1)S(1)}, bf16[2048,1024]{1,0:T(8,128)(2,1)}, u32[]{:S(2)}) copy-start(bf16[2048,1024]{1,0:T(8,128)(2,1)} %param.5) | copy-start | bytes 12582916
  63.7 2.0 copy-start
  71.7 70.0 %copy-start.1 = (s32[256]{0:T(256)S(1)}, s32[256]{0:T(256)}, u32[]{:S(2)}) copy-start(s32[256]{0:T(256)} %param.6) | copy-start | bytes 3076
  71.7 85.2 %copy-start.2 = (f32[256]{0:T(256)S(1)}, f32[256]{0:T(256)}, u32[]{:S(2)}) copy-start(f32[256]{0:T(256)} %param.7) | copy-start | bytes 3076
  71.7 120.2 %all-gather.2.cloned.1.call-start = ((), (), s32[]{:S(2)}) async-start(), calls=%async_computation.4 | async-start | bytes 2621440 | tf_op jit(solution)/shard_map/all_gather | solution.py:30
  159.3 132.8 %reduce-scatter.5.cloned.1.call-start = ((), (), s32[]{:S(2)}) async-start(), calls=%async_computation.5 | async-start | bytes 9437184 | tf_op jit(solution)/shard_map/reduce_scatter | solution.py:35
  202.4 1.6 copy-start.4
Sparse Core Ops, SparseCore 0:
  71.8 52.2 reduce-scatter.2
  159.4 32.3 all-gather.1
  202.6 89.5 reduce-scatter.4
